TPU v7x, 32 devices: a whole 2x2x4 slice. The times are simulated.
32 devices in a mesh: row: 8 (over z, x), col: 2 (over y), depth: 2 (over core).
Axes of the slice: x: 2, y: 2, z: 4, core: 2. Of those that a mesh axis runs over, the one named last changes fastest.
Arguments:
- tokens: bfloat16 [1024, 5376], P('row', 'depth'), may hold values from -6 to 6
- gate_weight: bfloat16 [9216, 5376], P(('col', 'row'), 'depth'), may hold values from -0.078125 to 0.078125
- up_weight: bfloat16 [9216, 5376], P(('col', 'row'), 'depth'), may hold values from -0.078125 to 0.078125
- down_weight: bfloat16 [9216, 5376], P(('col', 'depth'), 'row'), may hold values from -0.09375 to 0.09375
Outputs:
- output: bfloat16 [1024, 5376], P('row', ('col', 'depth'))
All inputs are finite; a program needn't handle non-finite values.
Results may differ from a plain program's by a relative error of at most 0.0049.
Values may be sent and summed in bfloat16 or wider, within the bound.
A program may use at most 128 MiB of HBM per device.

v0:
```python
import jax
import jax.numpy as jnp
from jax import lax
from jax.sharding import PartitionSpec as P


def local(tokens, gate_weight, up_weight, down_weight):
    paired = jnp.stack([gate_weight, up_weight])
    every_token = jnp.einsum(
        "td,gfd->gtf",
        lax.all_gather(tokens, "row", axis=0, tiled=True),
        paired,
        preferred_element_type=jnp.float32,
    )
    partial_sums = lax.all_to_all(every_token, "row", split_axis=1, concat_axis=2, tiled=True)
    share_width = partial_sums.shape[2] // lax.axis_size("depth")
    summed = lax.psum(partial_sums, "depth")
    shares = lax.dynamic_slice_in_dim(summed, lax.axis_index("depth") * share_width, share_width, 2)
    hidden = (jax.nn.silu(shares[0]) * shares[1]).astype(jnp.bfloat16)
    down_terms = jnp.dot(
        hidden,
        lax.all_gather(down_weight, "row", axis=1, tiled=True),
        preferred_element_type=jnp.float32,
    )
    return lax.psum_scatter(down_terms, ("col", "depth"), scatter_dimension=1, tiled=True).astype(
        jnp.bfloat16
    )


def solution(mesh):
    in_specs = (
        P("row", "depth"),
        P(("col", "row"), "depth"),
        P(("col", "row"), "depth"),
        P(("col", "depth"), "row"),
    )
    out_specs = P("row", ("col", "depth"))
    return jax.shard_map(local, mesh=mesh, in_specs=in_specs, out_specs=out_specs, check_vma=False)
```

profile of v0, /device:TPU:6, one launch (start us, length us, event | category | flops | bytes accessed | tf_op | source)
XLA Modules:
  0.0 808.3 jit_solution(2922904456121408201)
XLA Ops:
  6.5 0.0 all-gather.3.cloned.1.call-start
  6.5 0.7 all-gather.3.cloned.1.call-update
  7.3 0.0 all-reduce.2.cloned.1.call-start
  7.3 91.6 %all-gather.3.cloned.1.call-done = bf16[1024,2688]{1,0:T(8,128)(2,1)} async-done(((bf16[128,2688]{1,0:T(8,128)(2,1)}), bf16[1024,2688]{1,0:T(8,128)(2,1)}) %all-gather.3.cloned.1.call-update) | async-done | bytes 5505040 | tf_op jit(solution)/shard_map/all_gather | solution.py:11
  98.9 12.0 %fusion.5 = f32[2,1024,576]{1,2,0:T(8,128)} fusion(bf16[1024,2688]{1,0:T(8,128)(2,1)} %all-gather.3.cloned.1.call-done, bf16[1,576,2688]{2,1,0:T(8,128)(2,1)} %bitcast.29, bf16[1,576,2688]{2,1,0:T(8,128)(2,1)} %bitcast.30), kind=kOutput, calls=%fused_computation.5 | convolution fusion | flops 6344884224 | bytes 16416768 | tf_op jit(solution)/shard_map/td,gfd->gtf/dot_general | solution.py:9
  110.9 8.8 %copy.7 = f32[2,1024,576]{2,0,1:T(2,128)} copy(f32[2,1024,576]{1,2,0:T(8,128)} %fusion.5) | data formatting | bytes 9437184 | tf_op jit(solution)/shard_map/td,gfd->gtf/transpose | solution.py:9
  119.7 119.8 %all_to_all.18 = f32[2,1024,576]{2,0,1:T(2,128)} all-to-all(f32[2,1024,576]{2,0,1:T(2,128)} %copy.7), channel_id=1, replica_groups=mesh['row'=8,'col'=2,'depth'=2] {'row'}, dimensions={1} | all-to-all | bytes 9437184 | tf_op jit(solution)/shard_map/all_to_all | solution.py:15
  239.5 8.7 %copy.11 = f32[2,8,128,576]{2,3,1,0:T(8,128)} copy(f32[2,8,128,576]{3,0,2,1:T(2,128)} %bitcast.27) | data formatting | bytes 9437184 | tf_op jit(solution)/shard_map/all_to_all | solution.py:15
  248.2 0.0 all-reduce.2.cloned.1.call-update
  248.2 0.0 all-gather.5.cloned.1.call-start
  248.3 0.7 all-gather.5.cloned.1.call-update
  249.0 0.0 reduce-scatter.2.cloned.1.call-start
  249.0 27.5 %all-reduce.2.cloned.1.call-done = f32[2,128,4608]{1,2,0:T(8,128)} async-done(((f32[2,128,4608]{1,2,0:T(8,128)}), f32[2,128,4608]{1,2,0:T(8,128)}) %all-reduce.2.cloned.1.call-update) | async-done | bytes 4718608 | tf_op jit(solution)/shard_map/psum | solution.py:17
  276.5 474.6 %all-gather.5.cloned.1.call-done = bf16[2304,5376]{0,1:T(8,128)(2,1)} async-done(((bf16[2304,672]{0,1:T(8,128)(2,1)}), bf16[2304,5376]{0,1:T(8,128)(2,1)}) %all-gather.5.cloned.1.call-update) | async-done | bytes 24772624 | tf_op jit(solution)/shard_map/all_gather | solution.py:22
  751.1 13.3 %fusion.12 = f32[128,5376]{0,1:T(8,128)} fusion(bf16[2304,5376]{0,1:T(8,128)(2,1)} %all-gather.5.cloned.1.call-done, f32[2,128,4608]{1,2,0:T(8,128)} %all-reduce.2.cloned.1.call-done, s32[]{:T(128)S(6)} %add.13, s32[]{:T(128)S(6)} %select_n.3), kind=kOutput, calls=%fused_computation.10 | convolution fusion | flops 3172663296 | bytes 29884424 | tf_op jit(solution)/shard_map/dot_general | solution.py:20
  764.5 0.0 reduce-scatter.2.cloned.1.call-update
  764.5 35.4 %reduce-scatter.2.cloned.1.call-done = f32[128,1344]{0,1:T(8,128)} async-done(((f32[128,5376]{0,1:T(8,128)}), f32[128,1344]{0,1:T(8,128)}) %reduce-scatter.2.cloned.1.call-update) | async-done | bytes 688144 | tf_op jit(solution)/shard_map/reduce_scatter | solution.py:25
  799.9 1.9 convert_element_type.7
Async XLA Ops:
  6.5 92.4 %all-gather.3.cloned.1.call-start = ((), (), s32[]{:S(2)}) async-start(), calls=%async_computation.2 | async-start | bytes 6193152 | tf_op jit(solution)/shard_map/all_gather | solution.py:11
  7.3 269.3 %all-reduce.2.cloned.1.call-start = ((), (), s32[]{:S(2)}) async-start(), calls=%async_computation.3 | async-start | bytes 9437184 | tf_op jit(solution)/shard_map/psum | solution.py:17
  248.2 502.9 %all-gather.5.cloned.1.call-start = ((), (), s32[]{:S(2)}) async-start(), calls=%async_computation.4 | async-start | bytes 27869184 | tf_op jit(solution)/shard_map/all_gather | solution.py:22
  249.0 550.9 %reduce-scatter.2.cloned.1.call-start = ((), (), s32[]{:S(2)}) async-start(), calls=%async_computation.5 | async-start | bytes 3440640 | tf_op jit(solution)/shard_map/reduce_scatter | solution.py:25
Sparse Core Ops, SparseCore 0:
  9.5 89.3 all-gather.2
  248.3 28.1 all-reduce.1
  278.1 473.0 all-gather.4
  764.6 35.2 reduce-scatter.1
where the time goes:
time: 811 us; the launch traced here: 808 us
  waiting for transfers between devices  631 us (78%)
  blocking collectives  120 us (15%)
  matrix products  25.3 us (3%)
  local copies, waits for them, and re-layouts  17.5 us (2%)
  between operations  13.1 us (2%)
    all_gather x1, waiting for transfers between devices, local(): lax.all_gather(down_weight, 'row', axis=1, tiled=True)  475 us
    all_to_all x1, blocking collectives, local(): lax.all_to_all(every_token, 'row', split_axis=1, concat_axis=2, tiled=True)  120 us
    all_gather x1, waiting for transfers between devices, local(): lax.all_gather(tokens, 'row', axis=0, tiled=True)  91.6 us
    reduce_scatter x1, waiting for transfers between devices, local(): lax.psum_scatter(down_terms, ('col', 'depth'), scatter_dimension=1, tiled...  35.4 us
    psum x1, waiting for transfers between devices, local(): summed = lax.psum(partial_sums, 'depth')  27.5 us
  transfers between devices with their start and end apart: 4, of which 4 were waited for; matrix products, arithmetic and copies ran while one was open for 0% of the time, Pallas kernels for 0%

commit v1 on v0

v1 whole, which is shorter than its diff:
```python
import jax
import jax.numpy as jnp
from jax import lax
from jax.sharding import PartitionSpec as P


def send_out(partial, rows, cols, depths):
    quarters = cols * depths
    per = rows // quarters
    mine = lax.psum_scatter(partial, ("col", "depth"), scatter_dimension=0, tiled=True)
    mine = mine.astype(jnp.bfloat16)
    block = mine.shape[0] // per
    width = mine.shape[1]
    row = lax.axis_index("row")
    low = row % per
    got = jnp.zeros((block, per, width), jnp.bfloat16)
    for k in range(per):
        pairs = []
        for r in range(rows):
            for q in range(quarters):
                a, e = r // per, r % per
                to_row = q * per + (e + k) % per
                pairs.append((r * quarters + q, to_row * quarters + a))
        piece = lax.dynamic_slice_in_dim(mine, (low + k) % per * block, block, 0)
        piece = lax.ppermute(piece, ("row", "col", "depth"), pairs)
        got = lax.dynamic_update_slice_in_dim(got, piece[:, None], (low - k) % per, 1)
    return got.reshape(block, per * width)


def solution(mesh):
    rows, cols, depths = (mesh.shape[a] for a in ("row", "col", "depth"))

    def local(tokens, gate_weight, up_weight, down_weight):
        units = gate_weight.shape[0]
        every = lax.all_gather(tokens, "row", axis=0, tiled=True)
        down = down_weight.reshape(rows // depths, depths, units // depths, -1)
        down = lax.all_to_all(down, "depth", split_axis=1, concat_axis=0, tiled=True)
        down = down.reshape(rows, units // depths, -1)
        paired = jnp.stack([gate_weight, up_weight])
        sums = jnp.einsum("td,gfd->gtf", every, paired, preferred_element_type=jnp.float32)
        sums = lax.psum_scatter(sums, "depth", scatter_dimension=2, tiled=True)
        hidden = (jax.nn.silu(sums[0]) * sums[1]).astype(jnp.bfloat16)
        hidden = lax.all_gather(hidden, "row", axis=0)
        partial = jnp.einsum("rtk,rkc->tc", hidden, down, preferred_element_type=jnp.float32)
        return send_out(partial, rows, cols, depths)

    in_specs = (
        P("row", "depth"),
        P(("col", "row"), "depth"),
        P(("col", "row"), "depth"),
        P(("col", "depth"), "row"),
    )
    out_specs = P("row", ("col", "depth"))
    return jax.shard_map(local, mesh=mesh, in_specs=in_specs, out_specs=out_specs, check_vma=False)
```

time: 811 us -> 278 us (0.34)
  waiting for transfers between devices: 631 us -> 222 us
  blocking collectives: 120 us -> 6.58 us
  local copies, waits for them, and re-layouts: 17.5 us -> 5.53 us
    all_gather x2, waiting for transfers between devices: 566 us -> 160 us  [the longest x1 91.6 us: local(): every = lax.all_gather(tokens, 'row', axis=0, tiled=True)]
    all_to_all x1, blocking collectives: 120 us -> 6.58 us  [local(): lax.all_to_all(down, 'depth', split_axis=1, concat_axis=0, tiled=True)]
    psum x1 -> x0, waiting for transfers between devices: 27.5 us -> none  [local(): summed = lax.psum(partial_sums, 'depth')]
    ppermute x0 -> x2, waiting for transfers between devices: none -> 15.7 us  [send_out(): piece = lax.ppermute(piece, ('row', 'col', 'depth'), pairs)]
    reduce_scatter x1 -> x2, waiting for transfers between devices: 35.4 us -> 45.7 us  [the longest x1 33.7 us: send_out(): lax.psum_scatter(partial, ('col', 'depth'), scatter_dimension=0, tiled=True)]
    transpose x1 -> x0, local copies, waits for them, and re-layouts: 8.76 us -> none  [local(): jnp.einsum('td,gfd->gtf', lax.all_gather(tokens, 'row', axis=0, tiled=Tru...]
    all_to_all x1 -> x0, local copies, waits for them, and re-layouts: 8.69 us -> none  [local(): lax.all_to_all(every_token, 'row', split_axis=1, concat_axis=2, tiled=True)]
  transfers between devices with their start and end apart: 4 -> 6, of which waited for: 4 -> 6; matrix products, arithmetic and copies ran while one was open for 0% -> 2% of each run, Pallas kernels for 0% -> 0%
where the time goes in v1:
time: 278 us; the launch traced here: 276 us
  waiting for transfers between devices  222 us (80%)
  matrix products  19.3 us (7%)
  between operations  13.3 us (5%)
  blocking collectives  6.58 us (2%)
  starting transfers between devices  5.7 us (2%)
  local copies, waits for them, and re-layouts  5.53 us (2%)
  other arithmetic  3.94 us (1%)
    all_gather x1, waiting for transfers between devices, local(): every = lax.all_gather(tokens, 'row', axis=0, tiled=True)  91.6 us
    all_gather x1, waiting for transfers between devices, local(): hidden = lax.all_gather(hidden, 'row', axis=0)  68.1 us
    reduce_scatter x1, waiting for transfers between devices, send_out(): lax.psum_scatter(partial, ('col', 'depth'), scatter_dimension=0, tiled=True)  33.7 us
    ppermute x2, waiting for transfers between devices, send_out(): piece = lax.ppermute(piece, ('row', 'col', 'depth'), pairs)  15.7 us
    reduce_scatter x1, waiting for transfers between devices, local(): sums = lax.psum_scatter(sums, 'depth', scatter_dimension=2, tiled=True)  12.1 us
    dot_general x1, matrix products, local(): jnp.einsum('td,gfd->gtf', every, paired, preferred_element_type=jnp.float32)  12 us
    dot_general x1, matrix products, local(): jnp.einsum('rtk,rkc->tc', hidden, down, preferred_element_type=jnp.float32)  7.33 us
    all_to_all x1, blocking collectives, local(): lax.all_to_all(down, 'depth', split_axis=1, concat_axis=0, tiled=True)  6.58 us
  transfers between devices with their start and end apart: 6, of which 6 were waited for; matrix products, arithmetic and copies ran while one was open for 2% of the time, Pallas kernels for 0%

profile of v1, /device:TPU:6, one launch (start us, length us, event | category | flops | bytes accessed | tf_op | source)
XLA Modules:
  0.0 276.3 jit_solution(2160668187815438807)
XLA Ops:
  6.5 0.7 all-gather.3.cloned.1.call-update
  7.3 0.0 reduce-scatter.3.cloned.1.call-start
  7.3 91.6 %all-gather.3.cloned.1.call-done = bf16[1024,2688]{1,0:T(8,128)(2,1)} async-done(((bf16[128,2688]{1,0:T(8,128)(2,1)}), bf16[1024,2688]{1,0:T(8,128)(2,1)}) %all-gather.3.cloned.1.call-update) | async-done | bytes 5505040 | tf_op jit(solution)/shard_map/all_gather | solution.py:35
  98.9 12.0 %fusion.5 = f32[2,1024,576]{1,2,0:T(8,128)} fusion(bf16[1024,2688]{1,0:T(8,128)(2,1)} %all-gather.3.cloned.1.call-done, bf16[1,576,2688]{2,1,0:T(8,128)(2,1)} %bitcast.26, bf16[1,576,2688]{2,1,0:T(8,128)(2,1)} %bitcast.27), kind=kOutput, calls=%fused_computation.5 | convolution fusion | flops 6344884224 | bytes 16416768 | tf_op jit(solution)/shard_map/td,gfd->gtf/dot_general | solution.py:40
  110.9 0.0 reduce-scatter.3.cloned.1.call-update
  110.9 0.0 all-gather.5.cloned.1.call-start
  111.0 12.1 %reduce-scatter.3.cloned.1.call-done = f32[2,1024,288]{1,2,0:T(8,128)} async-done(((f32[2,1024,576]{1,2,0:T(8,128)}), f32[2,1024,288]{1,2,0:T(8,128)}) %reduce-scatter.3.cloned.1.call-update) | async-done | bytes 2359312 | tf_op jit(solution)/shard_map/reduce_scatter | solution.py:41
  123.1 2.8 %fusion.10 = bf16[1,1024,288]{1,2,0:T(8,128)(2,1)} fusion(f32[2,1024,288]{1,2,0:T(8,128)} %reduce-scatter.3.cloned.1.call-done), kind=kLoop, calls=%fused_computation.8 | loop fusion | flops 1769472 | bytes 2949120 | tf_op jit(solution)/shard_map/convert_element_type | solution.py:42
  125.9 0.0 all-gather.5.cloned.1.call-update
  125.9 0.0 reduce-scatter.5.cloned.1.call-start
  126.0 4.4 %copy.8 = bf16[2304,672]{1,0:T(8,128)(2,1)S(1)} copy(bf16[2304,672]{0,1:T(8,128)(2,1)} %param.7) | data formatting | bytes 6193152 | tf_op args[3]
  130.4 0.2 copy.9
  130.6 6.6 %all_to_all.15 = bf16[4,2,288,672]{3,2,0,1:T(8,128)(2,1)S(1)} all-to-all(bf16[4,2,288,672]{3,2,0,1:T(8,128)(2,1)S(1)} %copy.9), channel_id=1, replica_groups=mesh['row'=8,'col'=2,'depth'=2] {'depth'}, dimensions={1} | all-to-all | bytes 6193152 | tf_op jit(solution)/shard_map/all_to_all | solution.py:37
  137.2 68.1 %all-gather.5.cloned.1.call-done = bf16[8,1024,288]{1,2,0:T(8,128)(2,1)} async-done(((bf16[1,1024,288]{1,2,0:T(8,128)(2,1)}), bf16[8,1024,288]{1,2,0:T(8,128)(2,1)}) %all-gather.5.cloned.1.call-update) | async-done | bytes 4718608 | tf_op jit(solution)/shard_map/all_gather | solution.py:43
  205.4 7.3 %convolution_bitcast_fusion = f32[1024,672]{0,1:T(8,128)} fusion(bf16[8,1024,288]{1,2,0:T(8,128)(2,1)} %all-gather.5.cloned.1.call-done, bf16[8,288,672]{2,1,0:T(8,128)(2,1)S(1)} %bitcast.25), kind=kOutput, calls=%fused_computation.6 | convolution fusion | flops 3170893824 | bytes 10567680 | tf_op jit(solution)/shard_map/rtk,rkc->tc/dot_general | solution.py:44
  212.7 0.0 reduce-scatter.5.cloned.1.call-update
  212.8 33.7 %reduce-scatter.5.cloned.1.call-done = f32[256,672]{0,1:T(8,128)} async-done(((f32[1024,672]{0,1:T(8,128)}), f32[256,672]{0,1:T(8,128)}) %reduce-scatter.5.cloned.1.call-update) | async-done | bytes 688144 | tf_op jit(solution)/shard_map/reduce_scatter | solution.py:10
  246.4 1.1 convert_element_type.8
  247.6 5.2 %collective-permute-start = (bf16[128,672]{0,1:T(8,128)(2,1)S(1)}, bf16[128,672]{0,1:T(8,128)(2,1)S(1)}, u32[]{:S(2)}, u32[]{:S(2)}) collective-permute-start(bf16[128,672]{0,1:T(8,128)(2,1)S(1)} %get-tuple-element.6), channel_id=1, source_target_pairs={{0,0},{1,8},{2,16},{3,24},{4,4},{5,12},{6,20},{7,28},{8,1},{9,9},{... | collective-permute-start | bytes 516104 | tf_op jit(solution)/shard_map/ppermute | solution.py:25
  252.8 0.4 collective-permute-start.1
  253.2 12.4 %collective-permute-done = bf16[128,672]{0,1:T(8,128)(2,1)S(1)} collective-permute-done((bf16[128,672]{0,1:T(8,128)(2,1)S(1)}, bf16[128,672]{0,1:T(8,128)(2,1)S(1)}, u32[]{:S(2)}, u32[]{:S(2)}) %collective-permute-start) | collective-permute-done | bytes 172064 | tf_op jit(solution)/shard_map/ppermute | solution.py:25
  265.7 3.3 %collective-permute-done.1 = bf16[128,672]{0,1:T(8,128)(2,1)S(1)} collective-permute-done((bf16[128,672]{0,1:T(8,128)(2,1)S(1)}, bf16[128,672]{0,1:T(8,128)(2,1)S(1)}, u32[]{:S(2)}, u32[]{:S(2)}) %collective-permute-start.1) | collective-permute-done | bytes 172064 | tf_op jit(solution)/shard_map/ppermute | solution.py:25
  269.1 0.0 copy-start
  269.1 0.7 copy-done
  (5 shorter events, 0.1 us)
Async XLA Ops:
  6.5 92.4 %all-gather.3.cloned.1.call-start = ((), (), s32[]{:S(2)}) async-start(), calls=%async_computation.3 | async-start | bytes 6193152 | tf_op jit(solution)/shard_map/all_gather | solution.py:35
  7.3 115.8 %reduce-scatter.3.cloned.1.call-start = ((), (), s32[]{:S(2)}) async-start(), calls=%async_computation.4 | async-start | bytes 7077888 | tf_op jit(solution)/shard_map/reduce_scatter | solution.py:41
  110.9 94.4 %all-gather.5.cloned.1.call-start = ((), (), s32[]{:S(2)}) async-start(), calls=%async_computation.5 | async-start | bytes 5308416 | tf_op jit(solution)/shard_map/all_gather | solution.py:43
  125.9 120.5 %reduce-scatter.5.cloned.1.call-start = ((), (), s32[]{:S(2)}) async-start(), calls=%async_computation.6 | async-start | bytes 3440640 | tf_op jit(solution)/shard_map/reduce_scatter | solution.py:10
  247.6 18.0 %collective-permute-start = (bf16[128,672]{0,1:T(8,128)(2,1)S(1)}, bf16[128,672]{0,1:T(8,128)(2,1)S(1)}, u32[]{:S(2)}, u32[]{:S(2)}) collective-permute-start(bf16[128,672]{0,1:T(8,128)(2,1)S(1)} %get-tuple-element.6), channel_id=1, source_target_pairs={{0,0},{1,8},{2,16},{3,24},{4,4},{5,12},{6,20},{7,28},{8,1},{9,9},{... | collective-permute-start | bytes 516104 | tf_op jit(solution)/shard_map/ppermute | solution.py:25
  252.8 16.2 %collective-permute-start.1 = (bf16[128,672]{0,1:T(8,128)(2,1)S(1)}, bf16[128,672]{0,1:T(8,128)(2,1)S(1)}, u32[]{:S(2)}, u32[]{:S(2)}) collective-permute-start(bf16[128,672]{0,1:T(8,128)(2,1)S(1)} %get-tuple-element.5), channel_id=1, source_target_pairs={{0,4},{1,12},{2,20},{3,28},{4,0},{5,8},{6,16},{7,24},{8,5},{9,13},... | collective-permute-start | bytes 516104 | tf_op jit(solution)/shard_map/ppermute | solution.py:25
  269.1 0.7 copy-start
Sparse Core Ops, SparseCore 0:
  9.5 89.3 all-gather.2
  111.1 11.9 reduce-scatter.2
  126.0 79.2 all-gather.4
  212.8 33.5 reduce-scatter.4

commit v2 on v1

--- a/solution.py
+++ b/solution.py
@@ -1,14 +1,236 @@
+import functools
+
 import jax
 import jax.numpy as jnp
 from jax import lax
+from jax.experimental import pallas as pl
+from jax.experimental.pallas import tpu as pltpu
 from jax.sharding import PartitionSpec as P
 
-
-def send_out(partial, rows, cols, depths):
+MESH = pl.DeviceIdType.MESH
+F32 = jnp.float32
+BF16 = jnp.bfloat16
+
+
+def row_at(place, n):
+    back = place // (n // 2)
+    return 2 * place * (1 - back) + (2 * (n - 1 - place) + 1) * back
+
+
+def kernel(n, tok_hbm, gate_hbm, up_hbm, down_hbm, out_ref, tok, weights, down, part, theirs, hid,
+           total, other, send_y, from_y, load_sem, down_load, down_send, down_recv, tok_send, tok_recv,
+           y_send, y_recv, part_send, part_recv, hid_send, hid_recv, sum_send, sum_recv, col_send, col_recv):
+    row, col, core = lax.axis_index("row"), lax.axis_index("col"), lax.axis_index("depth")
+    half = n // 2
+    x, z = row % 2, row // 2
+    place = z * (1 - x) + (n - 1 - z) * x
+    ways = ({"row": row_at((place + 1) % n, n)}, {"row": row_at((place + n - 1) % n, n)})
+    beside, partner = {"col": 1 - col}, {"depth": 1 - core}
+    block = tok_hbm.shape[0]
+    third = tok_hbm.shape[1] // 3
+    units = gate_hbm.shape[0]
+    share = units // 2
+
+    def remote(src, dst, send, recv, to):
+        return pltpu.make_async_remote_copy(src_ref=src, dst_ref=dst, send_sem=send, recv_sem=recv,
+                                            device_id=to, device_id_type=MESH)
+
+    loads = [pltpu.make_async_copy(tok_hbm.at[:, pl.ds(t * third, third)], tok.at[t, 0], load_sem.at[t])
+             for t in range(3)]
+    loads += [pltpu.make_async_copy(gate_hbm, weights.at[0], load_sem.at[3]),
+              pltpu.make_async_copy(up_hbm, weights.at[1], load_sem.at[4])]
+    for copy in loads:
+        copy.start()
+    barrier = pltpu.get_barrier_semaphore()
+    for peer in ways + (beside, partner):
+        pl.semaphore_signal(barrier, inc=1, device_id=peer, device_id_type=MESH)
+    pl.semaphore_wait(barrier, 4)
+    for copy in loads[:3]:
+        copy.wait()
+
+    def slot(hop, way):
+        return 0 if hop == 0 else 1 if hop == half else 2 * hop + way
+
+    def rounds(hop, chunk):
+        return (chunk,) if hop == half else (0, 1)
+
+    started = []
+
+    def go(copy):
+        copy.start()
+        started.append(copy)
+
+    def tok_copy(hop, way, chunk):
+        t = 2 * col if chunk == 0 else 1
+        return remote(tok.at[t, slot(hop - 1, way)], tok.at[t, slot(hop, way)],
+                      tok_send.at[way, hop - 1, chunk], tok_recv.at[way, hop - 1, chunk], ways[way])
+
+    def y_copy(at, t):
+        return remote(tok.at[t, at], tok.at[t, at], y_send.at[at], y_recv.at[at], beside)
+
+    for chunk in (0, 1):
+        for way in (0, 1):
+            go(tok_copy(1, way, chunk))
+
+    local_down, remote_down = [], []
+    for i in range(half):
+        keep = down_hbm.at[pl.ds(i * units + core * share, share)]
+        give = down_hbm.at[pl.ds(i * units + (1 - core) * share, share)]
+        dst = down.at[core * half + i]
+        local_down.append(pltpu.make_async_copy(keep, dst, down_load.at[i]))
+        remote_down.append(remote(give, dst, down_send.at[i], down_recv.at[i], partner))
+    for copy in loads[3:]:
+        copy.wait()
+    for copy in local_down + remote_down:
+        copy.start()
+
+    def gate_up(group, slots, places):
+        wide = block * len(slots)
+        first = slots[0]
+
+        @pl.loop(0, 4)
+        def _(step):
+            side, kind = step // 2, step % 2
+            which = (1 - core) * (1 - side) + core * side
+            rows = pl.ds(pl.multiple_of(which * share, 16), share)
+            acc = None
+            for t in range(3):
+                seen = tok[t, first:first + len(slots)].reshape(wide, third)
+                term = lax.dot_general(weights[kind, rows, t * third:(t + 1) * third], seen,
+                                       (((1,), (1,)), ((), ())), preferred_element_type=F32)
+                acc = term if acc is None else acc + term
+            part[group, side, kind, :, :wide] = acc
+
+        swap = remote(part.at[group, 0, :, :, pl.ds(0, wide)], theirs.at[group, :, :, pl.ds(0, wide)],
+                      part_send.at[group], part_recv.at[group], partner)
+        go(swap)
+        swap.wait_recv()
+        for k, at in enumerate(places):
+            lanes = slice(k * block, (k + 1) * block)
+            gate = part[group, 1, 0, :, lanes] + theirs[group, 0, :, lanes]
+            up = part[group, 1, 1, :, lanes] + theirs[group, 1, :, lanes]
+            to = pl.ds(pl.multiple_of(row_at(at, n) * block, block), block)
+            hid[0, :, to] = (gate / (1.0 + jnp.exp(-gate)) * up).astype(BF16)
+
+    def pair(hop):
+        return [2 * hop, 2 * hop + 1], [(place + n - hop) % n, (place + hop) % n]
+
+    for hop in range(1, half + 1):
+        for chunk in (0, 1):
+            for way in rounds(hop, chunk):
+                tok_copy(hop, way, chunk).wait_recv()
+                if hop < half and way in rounds(hop + 1, chunk):
+                    go(tok_copy(hop + 1, way, chunk))
+                if chunk == 0:
+                    go(y_copy(slot(hop, way), 2 * col))
+        if hop == 1:
+            gate_up(0, [0], [place])
+        else:
+            slots, places = pair(hop - 1)
+            for at in slots:
+                y_copy(at, 2 - 2 * col).wait_recv()
+            gate_up(hop - 1, slots, places)
+    y_copy(1, 2 - 2 * col).wait_recv()
+    gate_up(half, [1], [(place + half) % n])
+
+    pieces = 2
+    lanes = block * n // pieces
+
+    def hid_copy(hop, way, chunk):
+        at = pl.ds(chunk * lanes, lanes)
+        return remote(hid.at[slot(hop - 1, way), :, at], hid.at[slot(hop, way), :, at],
+                      hid_send.at[way, hop - 1, chunk], hid_recv.at[way, hop - 1, chunk], ways[way])
+
+    for chunk in range(pieces):
+        for way in (0, 1):
+            go(hid_copy(1, way, chunk))
+    for copy in local_down:
+        copy.wait()
+    for copy in remote_down:
+        copy.wait()
+
+    quarter = total.shape[1]
+
+    def add_down(at, source, start):
+        of = row_at(source, n)
+
+        @pl.loop(0, total.shape[0])
+        def _(q):
+            some = hid[at, :, pl.ds(pl.multiple_of(q * quarter, quarter), quarter)]
+            term = lax.dot_general(some, down[of], (((0,), (0,)), ((), ())), preferred_element_type=F32)
+            total[q] = term if start else total[q] + term
+
+    add_down(0, place, True)
+    for hop in range(1, half + 1):
+        for chunk in range(pieces):
+            for way in rounds(hop, chunk):
+                hid_copy(hop, way, chunk).wait_recv()
+                if hop < half and way in rounds(hop + 1, chunk):
+                    go(hid_copy(hop + 1, way, chunk))
+        if hop < half:
+            slots, places = pair(hop)
+            for at, source in zip(slots, places):
+                add_down(at, source, False)
+    add_down(1, (place + half) % n, False)
+
+    def sum_copy(c, k):
+        return remote(total.at[c * 2 + 1 - core], other.at[c], sum_send.at[k], sum_recv.at[k], partner)
+
+    go(sum_copy(1 - col, 0))
+    go(sum_copy(col, 1))
+    sum_copy(1 - col, 0).wait_recv()
+    send_y[...] = (total[(1 - col) * 2 + core] + other[1 - col]).astype(BF16)
+    swap = remote(send_y, from_y, col_send, col_recv, beside)
+    go(swap)
+    sum_copy(col, 1).wait_recv()
+    mine = total[col * 2 + core] + other[col]
+    swap.wait_recv()
+    out_ref[...] = (mine + from_y[...].astype(F32)).astype(BF16)
+    for copy in started:
+        copy.wait_send()
+
+
+def partial_sums(n, tokens, gate_weight, up_weight, down_weight):
+    block, width = tokens.shape
+    units = gate_weight.shape[0]
+    features = down_weight.shape[1]
+    half, share = n // 2, units // 2
+    every = n * block
+    dma = pltpu.SemaphoreType.DMA
+    return pl.pallas_call(
+        functools.partial(kernel, n),
+        out_shape=jax.ShapeDtypeStruct((every // 4, features), BF16),
+        in_specs=[pl.BlockSpec(memory_space=pl.ANY)] * 4,
+        out_specs=pl.BlockSpec(memory_space=pltpu.VMEM),
+        scratch_shapes=[
+            pltpu.VMEM((3, n, block, width // 3), BF16),
+            pltpu.VMEM((2, units, width), BF16),
+            pltpu.VMEM((n, share, features), BF16),
+            pltpu.VMEM((half + 1, 2, 2, share, 2 * block), F32),
+            pltpu.VMEM((half + 1, 2, share, 2 * block), F32),
+            pltpu.VMEM((n, share, every), BF16),
+            pltpu.VMEM((4, every // 4, features), F32),
+            pltpu.VMEM((2, every // 4, features), F32),
+            pltpu.VMEM((every // 4, features), BF16),
+            pltpu.VMEM((every // 4, features), BF16),
+            dma((5,)),
+            dma((half,)), dma((half,)), dma((half,)),
+            dma((2, half, 2)), dma((2, half, 2)),
+            dma((n,)), dma((n,)),
+            dma((half + 1,)), dma((half + 1,)),
+            dma((2, half, 2)), dma((2, half, 2)),
+            dma((2,)), dma((2,)),
+            dma, dma,
+        ],
+        compiler_params=pltpu.CompilerParams(
+            collective_id=0, has_side_effects=True, vmem_limit_bytes=60 * 1024 * 1024
+        ),
+    )(tokens, gate_weight, up_weight, down_weight)
+
+
+def send_out(mine, rows, cols, depths):
     quarters = cols * depths
     per = rows // quarters
-    mine = lax.psum_scatter(partial, ("col", "depth"), scatter_dimension=0, tiled=True)
-    mine = mine.astype(jnp.bfloat16)
     block = mine.shape[0] // per
     width = mine.shape[1]
     row = lax.axis_index("row")
@@ -42,7 +264,11 @@
         hidden = (jax.nn.silu(sums[0]) * sums[1]).astype(jnp.bfloat16)
         hidden = lax.all_gather(hidden, "row", axis=0)
         partial = jnp.einsum("rtk,rkc->tc", hidden, down, preferred_element_type=jnp.float32)
-        return send_out(partial, rows, cols, depths)
+        mine = lax.psum_scatter(partial, ("col", "depth"), scatter_dimension=0, tiled=True)
+        return send_out(mine.astype(BF16), rows, cols, depths)
+
+    def fused(*args):
+        return send_out(partial_sums(rows, *args), rows, cols, depths)
 
     in_specs = (
         P("row", "depth"),
@@ -51,4 +277,5 @@
         P(("col", "depth"), "row"),
     )
     out_specs = P("row", ("col", "depth"))
-    return jax.shard_map(local, mesh=mesh, in_specs=in_specs, out_specs=out_specs, check_vma=False)
+    small = cols == 2 and depths == 2 and rows % 4 == 0
+    return jax.shard_map(fused if small else local, mesh=mesh, in_specs=in_specs, out_specs=out_specs, check_vma=False)

time: 278 us -> 145 us (0.52)
  waiting for transfers between devices: 222 us -> 17.5 us
  Pallas kernels: 0 us -> 112 us
  matrix products: 19.3 us -> 0 us
  between operations: 13.3 us -> 0.06 us
  blocking collectives: 6.58 us -> 0 us
  other arithmetic: 3.94 us -> 0 us
    all_gather x2 -> x0, waiting for transfers between devices: 160 us -> none  [the longest x1 91.6 us: local(): every = lax.all_gather(tokens, 'row', axis=0, tiled=True)]
    pallas_call x0 -> x1, Pallas kernels: none -> 112 us  [partial_sums(): pl.pallas_call(functools.partial(kernel, n), out_shape=jax.ShapeDtypeStru...]
    reduce_scatter x2 -> x0, waiting for transfers between devices: 45.7 us -> none  [the longest x1 33.7 us: send_out(): lax.psum_scatter(partial, ('col', 'depth'), scatter_dimension=0, tiled=True)]
    dot_general x2 -> x0, matrix products: 19.3 us -> none  [the longest x1 12 us: local(): jnp.einsum('td,gfd->gtf', every, paired, preferred_element_type=jnp.float32)]
    all_to_all x1 -> x0, blocking collectives: 6.58 us -> none  [local(): lax.all_to_all(down, 'depth', split_axis=1, concat_axis=0, tiled=True)]
    convert_element_type x2 -> x0, other arithmetic: 3.94 us -> none  [the longest x1 2.81 us: local(): hidden = (jax.nn.silu(sums[0]) * sums[1]).astype(jnp.bfloat16)]
  transfers between devices with their start and end apart: 6 -> 2, of which waited for: 6 -> 2; matrix products, arithmetic and copies ran while one was open for 2% -> 0% of each run, Pallas kernels for 0% -> 0%
where the time goes in v2:
time: 145 us; the launch traced here: 144 us
  Pallas kernels  112 us (77%)
  waiting for transfers between devices  17.5 us (12%)
  local copies, waits for them, and re-layouts  7.82 us (5%)
  starting transfers between devices  7.13 us (5%)
    pallas_call x1, Pallas kernels, partial_sums(): pl.pallas_call(functools.partial(kernel, n), out_shape=jax.ShapeDtypeStru...  112 us
    ppermute x2, waiting for transfers between devices, send_out(): piece = lax.ppermute(piece, ('row', 'col', 'depth'), pairs)  17.5 us
    ppermute x2, starting transfers between devices, send_out(): piece = lax.ppermute(piece, ('row', 'col', 'depth'), pairs)  7.13 us
    unnamed x3, local copies, waits for them, and re-layouts  6.31 us
  transfers between devices with their start and end apart: 2, of which 2 were waited for; matrix products, arithmetic and copies ran while one was open for 0% of the time, Pallas kernels for 0%

profile of v2, /device:TPU:6, one launch (start us, length us, event | category | flops | bytes accessed | tf_op | source)
XLA Modules:
  0.0 144.4 jit_solution(2522716540508715796)
XLA Ops:
  0.0 5.6 %copy.5.down_hbm = bf16[2304,672]{1,0:T(8,128)(2,1)} copy(bf16[2304,672]{0,1:T(8,128)(2,1)} %param.7) | data formatting | bytes 6193152 | tf_op args[3]
  5.6 111.9 %shard_map.46 = bf16[256,672]{1,0:T(8,128)(2,1)} custom-call(bf16[128,2688]{1,0:T(8,128)(2,1)} %tok_hbm.1, bf16[576,2688]{1,0:T(8,128)(2,1)} %gate_hbm.1, bf16[576,2688]{1,0:T(8,128)(2,1)} %up_hbm.1, bf16[2304,672]{1,0:T(8,128)(2,1)} %copy.5.down_hbm), custom_call_target="tpu_custom_call" | custom-call | tf_op jit(solution)/shard_map/pallas_call | solution.py:200
  117.5 1.1 constant_dynamic-slice_fusion
  118.5 4.3 %collective-permute-start = (bf16[128,672]{1,0:T(8,128)(2,1)S(1)}, bf16[128,672]{1,0:T(8,128)(2,1)S(1)}, u32[]{:S(2)}, u32[]{:S(2)}) collective-permute-start(bf16[128,672]{1,0:T(8,128)(2,1)S(1)} %get-tuple-element.6), channel_id=1, source_target_pairs={{0,0},{1,8},{2,16},{3,24},{4,4},{5,12},{6,20},{7,28},{8,1},{9,9},{... | collective-permute-start | bytes 516104 | tf_op jit(solution)/shard_map/ppermute | solution.py:247
  122.9 2.8 %collective-permute-start.1 = (bf16[128,672]{1,0:T(8,128)(2,1)S(1)}, bf16[128,672]{1,0:T(8,128)(2,1)S(1)}, u32[]{:S(2)}, u32[]{:S(2)}) collective-permute-start(bf16[128,672]{1,0:T(8,128)(2,1)S(1)} %get-tuple-element.5), channel_id=1, source_target_pairs={{0,4},{1,12},{2,20},{3,28},{4,0},{5,8},{6,16},{7,24},{8,5},{9,13},... | collective-permute-start | bytes 516104 | tf_op jit(solution)/shard_map/ppermute | solution.py:247
  125.7 12.8 %collective-permute-done = bf16[128,672]{1,0:T(8,128)(2,1)S(1)} collective-permute-done((bf16[128,672]{1,0:T(8,128)(2,1)S(1)}, bf16[128,672]{1,0:T(8,128)(2,1)S(1)}, u32[]{:S(2)}, u32[]{:S(2)}) %collective-permute-start) | collective-permute-done | bytes 172064 | tf_op jit(solution)/shard_map/ppermute | solution.py:247
  138.5 0.2 copy.6
  138.7 4.7 %collective-permute-done.1 = bf16[128,672]{1,0:T(8,128)(2,1)S(1)} collective-permute-done((bf16[128,672]{1,0:T(8,128)(2,1)S(1)}, bf16[128,672]{1,0:T(8,128)(2,1)S(1)}, u32[]{:S(2)}, u32[]{:S(2)}) %collective-permute-start.1) | collective-permute-done | bytes 172064 | tf_op jit(solution)/shard_map/ppermute | solution.py:247
  143.4 0.2 copy.7
  143.6 0.0 copy-start
  143.7 0.7 copy-done
  (3 shorter events, 0.1 us)
Async XLA Ops:
  118.5 19.9 %collective-permute-start = (bf16[128,672]{1,0:T(8,128)(2,1)S(1)}, bf16[128,672]{1,0:T(8,128)(2,1)S(1)}, u32[]{:S(2)}, u32[]{:S(2)}) collective-permute-start(bf16[128,672]{1,0:T(8,128)(2,1)S(1)} %get-tuple-element.6), channel_id=1, source_target_pairs={{0,0},{1,8},{2,16},{3,24},{4,4},{5,12},{6,20},{7,28},{8,1},{9,9},{... | collective-permute-start | bytes 516104 | tf_op jit(solution)/shard_map/ppermute | solution.py:247
  122.9 20.6 %collective-permute-start.1 = (bf16[128,672]{1,0:T(8,128)(2,1)S(1)}, bf16[128,672]{1,0:T(8,128)(2,1)S(1)}, u32[]{:S(2)}, u32[]{:S(2)}) collective-permute-start(bf16[128,672]{1,0:T(8,128)(2,1)S(1)} %get-tuple-element.5), channel_id=1, source_target_pairs={{0,4},{1,12},{2,20},{3,28},{4,0},{5,8},{6,16},{7,24},{8,5},{9,13},... | collective-permute-start | bytes 516104 | tf_op jit(solution)/shard_map/ppermute | solution.py:247
  143.6 0.7 copy-start

commit v3 on v2

--- a/solution.py
+++ b/solution.py
@@ -17,7 +17,7 @@
     return 2 * place * (1 - back) + (2 * (n - 1 - place) + 1) * back
 
 
-def kernel(n, tok_hbm, gate_hbm, up_hbm, down_hbm, out_ref, tok, weights, down, part, theirs, hid,
+def kernel(n, tok_hbm, gate_hbm, up_hbm, down_hbm, out_ref, tok, weights, turned, rows_of, down, part, theirs, hid,
            total, other, send_y, from_y, load_sem, down_load, down_send, down_recv, tok_send, tok_recv,
            y_send, y_recv, part_send, part_recv, hid_send, hid_recv, sum_send, sum_recv, col_send, col_recv):
     row, col, core = lax.axis_index("row"), lax.axis_index("col"), lax.axis_index("depth")
@@ -38,7 +38,8 @@
     loads = [pltpu.make_async_copy(tok_hbm.at[:, pl.ds(t * third, third)], tok.at[t, 0], load_sem.at[t])
              for t in range(3)]
     loads += [pltpu.make_async_copy(gate_hbm, weights.at[0], load_sem.at[3]),
-              pltpu.make_async_copy(up_hbm, weights.at[1], load_sem.at[4])]
+              pltpu.make_async_copy(up_hbm, weights.at[1], load_sem.at[4]),
+              pltpu.make_async_copy(down_hbm, turned, load_sem.at[5])]
     for copy in loads:
         copy.start()
     barrier = pltpu.get_barrier_semaphore()
@@ -74,17 +75,23 @@
 
     local_down, remote_down = [], []
     for i in range(half):
-        keep = down_hbm.at[pl.ds(i * units + core * share, share)]
-        give = down_hbm.at[pl.ds(i * units + (1 - core) * share, share)]
+        keep = rows_of.at[pl.ds(i * units + core * share, share)]
+        give = rows_of.at[pl.ds(i * units + (1 - core) * share, share)]
         dst = down.at[core * half + i]
         local_down.append(pltpu.make_async_copy(keep, dst, down_load.at[i]))
         remote_down.append(remote(give, dst, down_send.at[i], down_recv.at[i], partner))
     for copy in loads[3:]:
         copy.wait()
+
+    @pl.loop(0, turned.shape[1] // 128)
+    def _(step):
+        at = pl.ds(pl.multiple_of(step * 128, 128), 128)
+        rows_of[at, :] = turned[:, at].T
+
     for copy in local_down + remote_down:
         copy.start()
 
-    def gate_up(group, slots, places):
+    def gate_up(group, slots, to):
         wide = block * len(slots)
         first = slots[0]
 
@@ -105,16 +112,51 @@
                       part_send.at[group], part_recv.at[group], partner)
         go(swap)
         swap.wait_recv()
-        for k, at in enumerate(places):
-            lanes = slice(k * block, (k + 1) * block)
-            gate = part[group, 1, 0, :, lanes] + theirs[group, 0, :, lanes]
-            up = part[group, 1, 1, :, lanes] + theirs[group, 1, :, lanes]
-            to = pl.ds(pl.multiple_of(row_at(at, n) * block, block), block)
-            hid[0, :, to] = (gate / (1.0 + jnp.exp(-gate)) * up).astype(BF16)
-
-    def pair(hop):
-        return [2 * hop, 2 * hop + 1], [(place + n - hop) % n, (place + hop) % n]
-
+        gate = part[group, 1, 0, :, :wide] + theirs[group, 0, :, :wide]
+        up = part[group, 1, 1, :, :wide] + theirs[group, 1, :, :wide]
+        hid[0, :, to:to + wide] = (gate / (1.0 + jnp.exp(-gate)) * up).astype(BF16)
+
+    wide_piece = 2 * block
+
+    def hid_copy(piece, hop, way):
+        at = pl.ds((piece - 1) * wide_piece, wide_piece)
+        return remote(hid.at[slot(hop - 1, way), :, at], hid.at[slot(hop, way), :, at],
+                      hid_send.at[way, hop - 1, piece - 1], hid_recv.at[way, hop - 1, piece - 1], ways[way])
+
+    def hid_rounds(piece, hop):
+        return (piece % 2,) if hop == half else (0, 1)
+
+    def add_down(at, source, piece):
+        lanes = slice((piece - 1) * wide_piece, piece * wide_piece)
+        term = lax.dot_general(hid[at, :, lanes], down[row_at(source, n)], (((0,), (0,)), ((), ())),
+                               preferred_element_type=F32)
+        before = source if piece == half else (source + n - piece) % n
+        for k, token_block in enumerate((before, (source + piece) % n)):
+            total[row_at(token_block, n)] += term[k * block:(k + 1) * block]
+
+    def wave(number):
+        for piece in range(1, half + 1):
+            hop = number + 1 - piece
+            if hop == 1:
+                for way in (0, 1):
+                    go(hid_copy(piece, 1, way))
+            elif 2 <= hop <= half + 1:
+                for way in hid_rounds(piece, hop - 1):
+                    hid_copy(piece, hop - 1, way).wait_recv()
+                    if hop <= half and way in hid_rounds(piece, hop):
+                        go(hid_copy(piece, hop, way))
+        for piece in range(1, half + 1):
+            hop = number - piece
+            if hop == 0:
+                add_down(0, place, piece)
+            elif hop == half:
+                add_down(1, (place + half) % n, piece)
+            elif 1 <= hop < half:
+                @pl.loop(0, 2)
+                def _(way):
+                    add_down(2 * hop + way, (place + n - hop + 2 * hop * way) % n, piece)
+
+    total[...] = jnp.zeros_like(total)
     for hop in range(1, half + 1):
         for chunk in (0, 1):
             for way in rounds(hop, chunk):
@@ -124,68 +166,44 @@
                 if chunk == 0:
                     go(y_copy(slot(hop, way), 2 * col))
         if hop == 1:
-            gate_up(0, [0], [place])
+            gate_up(0, [0], (half - 1) * wide_piece)
+            for copy in local_down:
+                copy.wait()
+            for copy in remote_down:
+                copy.wait()
         else:
-            slots, places = pair(hop - 1)
+            slots = [2 * (hop - 1), 2 * (hop - 1) + 1]
             for at in slots:
                 y_copy(at, 2 - 2 * col).wait_recv()
-            gate_up(hop - 1, slots, places)
+            gate_up(hop - 1, slots, (hop - 2) * wide_piece)
+            wave(hop - 1)
     y_copy(1, 2 - 2 * col).wait_recv()
-    gate_up(half, [1], [(place + half) % n])
-
-    pieces = 2
-    lanes = block * n // pieces
-
-    def hid_copy(hop, way, chunk):
-        at = pl.ds(chunk * lanes, lanes)
-        return remote(hid.at[slot(hop - 1, way), :, at], hid.at[slot(hop, way), :, at],
-                      hid_send.at[way, hop - 1, chunk], hid_recv.at[way, hop - 1, chunk], ways[way])
-
-    for chunk in range(pieces):
-        for way in (0, 1):
-            go(hid_copy(1, way, chunk))
-    for copy in local_down:
-        copy.wait()
-    for copy in remote_down:
-        copy.wait()
-
-    quarter = total.shape[1]
-
-    def add_down(at, source, start):
-        of = row_at(source, n)
-
-        @pl.loop(0, total.shape[0])
-        def _(q):
-            some = hid[at, :, pl.ds(pl.multiple_of(q * quarter, quarter), quarter)]
-            term = lax.dot_general(some, down[of], (((0,), (0,)), ((), ())), preferred_element_type=F32)
-            total[q] = term if start else total[q] + term
-
-    add_down(0, place, True)
-    for hop in range(1, half + 1):
-        for chunk in range(pieces):
-            for way in rounds(hop, chunk):
-                hid_copy(hop, way, chunk).wait_recv()
-                if hop < half and way in rounds(hop + 1, chunk):
-                    go(hid_copy(hop + 1, way, chunk))
-        if hop < half:
-            slots, places = pair(hop)
-            for at, source in zip(slots, places):
-                add_down(at, source, False)
-    add_down(1, (place + half) % n, False)
-
-    def sum_copy(c, k):
-        return remote(total.at[c * 2 + 1 - core], other.at[c], sum_send.at[k], sum_recv.at[k], partner)
-
-    go(sum_copy(1 - col, 0))
-    go(sum_copy(col, 1))
-    sum_copy(1 - col, 0).wait_recv()
-    send_y[...] = (total[(1 - col) * 2 + core] + other[1 - col]).astype(BF16)
-    swap = remote(send_y, from_y, col_send, col_recv, beside)
-    go(swap)
-    sum_copy(col, 1).wait_recv()
-    mine = total[col * 2 + core] + other[col]
-    swap.wait_recv()
-    out_ref[...] = (mine + from_y[...].astype(F32)).astype(BF16)
+    gate_up(half, [1], (half - 1) * wide_piece + block)
+    for number in range(half, 2 * half + 1):
+        wave(number)
+
+    few = n // 4
+
+    def sum_copy(side, k):
+        c = 1 - col if side == 0 else col
+        return remote(total.at[(c * 2 + 1 - core) * few + k], other.at[side, k],
+                      sum_send.at[side, k], sum_recv.at[side, k], partner)
+
+    def col_copy(k):
+        return remote(send_y.at[k], from_y.at[k], col_send.at[k], col_recv.at[k], beside)
+
+    for side in (0, 1):
+        for k in range(few):
+            go(sum_copy(side, k))
+    for k in range(few):
+        sum_copy(0, k).wait_recv()
+        send_y[k] = (total[((1 - col) * 2 + core) * few + k] + other[0, k]).astype(BF16)
+        go(col_copy(k))
+    for k in range(few):
+        sum_copy(1, k).wait_recv()
+        mine = total[(col * 2 + core) * few + k] + other[1, k]
+        col_copy(k).wait_recv()
+        out_ref[k * block:(k + 1) * block] = (mine + from_y[k].astype(F32)).astype(BF16)
     for copy in started:
         copy.wait_send()
 
@@ -194,6 +212,7 @@
     block, width = tokens.shape
     units = gate_weight.shape[0]
     features = down_weight.shape[1]
+    few = n // 4
     half, share = n // 2, units // 2
     every = n * block
     dma = pltpu.SemaphoreType.DMA
@@ -205,27 +224,29 @@
         scratch_shapes=[
             pltpu.VMEM((3, n, block, width // 3), BF16),
             pltpu.VMEM((2, units, width), BF16),
+            pltpu.VMEM((features, down_weight.shape[0]), BF16),
+            pltpu.VMEM((down_weight.shape[0], features), BF16),
             pltpu.VMEM((n, share, features), BF16),
             pltpu.VMEM((half + 1, 2, 2, share, 2 * block), F32),
             pltpu.VMEM((half + 1, 2, share, 2 * block), F32),
             pltpu.VMEM((n, share, every), BF16),
-            pltpu.VMEM((4, every // 4, features), F32),
-            pltpu.VMEM((2, every // 4, features), F32),
-            pltpu.VMEM((every // 4, features), BF16),
-            pltpu.VMEM((every // 4, features), BF16),
-            dma((5,)),
+            pltpu.VMEM((n, block, features), F32),
+            pltpu.VMEM((2, few, block, features), F32),
+            pltpu.VMEM((few, block, features), BF16),
+            pltpu.VMEM((few, block, features), BF16),
+            dma((6,)),
             dma((half,)), dma((half,)), dma((half,)),
             dma((2, half, 2)), dma((2, half, 2)),
             dma((n,)), dma((n,)),
             dma((half + 1,)), dma((half + 1,)),
-            dma((2, half, 2)), dma((2, half, 2)),
-            dma((2,)), dma((2,)),
-            dma, dma,
+            dma((2, half, half)), dma((2, half, half)),
+            dma((2, few)), dma((2, few)),
+            dma((few,)), dma((few,)),
         ],
         compiler_params=pltpu.CompilerParams(
             collective_id=0, has_side_effects=True, vmem_limit_bytes=60 * 1024 * 1024
         ),
-    )(tokens, gate_weight, up_weight, down_weight)
+    )(tokens, gate_weight, up_weight, down_weight.T)
 
 
 def send_out(mine, rows, cols, depths):

time: 145 us -> 125 us (0.86)
  Pallas kernels: 112 us -> 99.6 us
  local copies, waits for them, and re-layouts: 7.82 us -> 2.23 us
  waiting for transfers between devices: 17.5 us -> 15.2 us
    pallas_call x1, Pallas kernels: 112 us -> 99.6 us  [partial_sums(): pl.pallas_call(functools.partial(kernel, n), out_shape=jax.ShapeDtypeStru...]
    unnamed x3 -> x2, local copies, waits for them, and re-layouts: 6.31 us -> 0.72 us
    ppermute x2, waiting for transfers between devices: 17.5 us -> 15.2 us  [send_out(): piece = lax.ppermute(piece, ('row', 'col', 'depth'), pairs)]
where the time goes in v3:
time: 125 us
  Pallas kernels  99.6 us (80%)
  waiting for transfers between devices  15.2 us (12%)
  starting transfers between devices  7.74 us (6%)
  local copies, waits for them, and re-layouts  2.23 us (2%)
    pallas_call x1, Pallas kernels, partial_sums(): pl.pallas_call(functools.partial(kernel, n), out_shape=jax.ShapeDtypeStru...  99.6 us
    ppermute x2, waiting for transfers between devices, send_out(): piece = lax.ppermute(piece, ('row', 'col', 'depth'), pairs)  15.2 us
    ppermute x2, starting transfers between devices, send_out(): piece = lax.ppermute(piece, ('row', 'col', 'depth'), pairs)  7.74 us
  transfers between devices with their start and end apart: 2, of which 2 were waited for; matrix products, arithmetic and copies ran while one was open for 0% of the time, Pallas kernels for 0%

profile of v3, /device:TPU:6, one launch (start us, length us, event | category | flops | bytes accessed | tf_op | source)
XLA Modules:
  0.0 124.9 jit_solution(16486337438356625114)
XLA Ops:
  0.0 99.6 %shard_map.46 = bf16[256,672]{1,0:T(8,128)(2,1)} custom-call(bf16[128,2688]{1,0:T(8,128)(2,1)} %tok_hbm.1, bf16[576,2688]{1,0:T(8,128)(2,1)} %gate_hbm.1, bf16[576,2688]{1,0:T(8,128)(2,1)} %up_hbm.1, bf16[672,2304]{1,0:T(8,128)(2,1)} %bitcast.5), custom_call_target="tpu_custom_call" | custom-call | tf_op jit(solution)/shard_map/pallas_call | solution.py:219
  99.6 1.1 constant_dynamic-slice_fusion
  100.7 2.3 %collective-permute-start.1 = (bf16[128,672]{1,0:T(8,128)(2,1)S(1)}, bf16[128,672]{1,0:T(8,128)(2,1)S(1)}, u32[]{:S(2)}, u32[]{:S(2)}) collective-permute-start(bf16[128,672]{1,0:T(8,128)(2,1)S(1)} %get-tuple-element.5), channel_id=1, source_target_pairs={{0,4},{1,12},{2,20},{3,28},{4,0},{5,8},{6,16},{7,24},{8,5},{9,13},... | collective-permute-start | bytes 516104 | tf_op jit(solution)/shard_map/ppermute | solution.py:268
  103.0 5.5 %collective-permute-start = (bf16[128,672]{1,0:T(8,128)(2,1)S(1)}, bf16[128,672]{1,0:T(8,128)(2,1)S(1)}, u32[]{:S(2)}, u32[]{:S(2)}) collective-permute-start(bf16[128,672]{1,0:T(8,128)(2,1)S(1)} %get-tuple-element.6), channel_id=1, source_target_pairs={{0,0},{1,8},{2,16},{3,24},{4,4},{5,12},{6,20},{7,28},{8,1},{9,9},{... | collective-permute-start | bytes 516104 | tf_op jit(solution)/shard_map/ppermute | solution.py:268
  108.5 10.4 %collective-permute-done.1 = bf16[128,672]{1,0:T(8,128)(2,1)S(1)} collective-permute-done((bf16[128,672]{1,0:T(8,128)(2,1)S(1)}, bf16[128,672]{1,0:T(8,128)(2,1)S(1)}, u32[]{:S(2)}, u32[]{:S(2)}) %collective-permute-start.1) | collective-permute-done | bytes 172064 | tf_op jit(solution)/shard_map/ppermute | solution.py:268
  118.9 0.2 copy.6
  119.1 4.7 %collective-permute-done = bf16[128,672]{1,0:T(8,128)(2,1)S(1)} collective-permute-done((bf16[128,672]{1,0:T(8,128)(2,1)S(1)}, bf16[128,672]{1,0:T(8,128)(2,1)S(1)}, u32[]{:S(2)}, u32[]{:S(2)}) %collective-permute-start) | collective-permute-done | bytes 172064 | tf_op jit(solution)/shard_map/ppermute | solution.py:268
  123.9 0.2 copy.5
  124.1 0.0 copy-start
  124.2 0.7 copy-done
  (3 shorter events, 0.1 us)
Async XLA Ops:
  100.7 18.2 %collective-permute-start.1 = (bf16[128,672]{1,0:T(8,128)(2,1)S(1)}, bf16[128,672]{1,0:T(8,128)(2,1)S(1)}, u32[]{:S(2)}, u32[]{:S(2)}) collective-permute-start(bf16[128,672]{1,0:T(8,128)(2,1)S(1)} %get-tuple-element.5), channel_id=1, source_target_pairs={{0,4},{1,12},{2,20},{3,28},{4,0},{5,8},{6,16},{7,24},{8,5},{9,13},... | collective-permute-start | bytes 516104 | tf_op jit(solution)/shard_map/ppermute | solution.py:268
  103.0 20.9 %collective-permute-start = (bf16[128,672]{1,0:T(8,128)(2,1)S(1)}, bf16[128,672]{1,0:T(8,128)(2,1)S(1)}, u32[]{:S(2)}, u32[]{:S(2)}) collective-permute-start(bf16[128,672]{1,0:T(8,128)(2,1)S(1)} %get-tuple-element.6), channel_id=1, source_target_pairs={{0,0},{1,8},{2,16},{3,24},{4,4},{5,12},{6,20},{7,28},{8,1},{9,9},{... | collective-permute-start | bytes 516104 | tf_op jit(solution)/shard_map/ppermute | solution.py:268
  124.1 0.7 copy-start

commit v4 on v3

--- a/solution.py
+++ b/solution.py
@@ -19,7 +19,8 @@
 
 def kernel(n, tok_hbm, gate_hbm, up_hbm, down_hbm, out_ref, tok, weights, turned, rows_of, down, part, theirs, hid,
            total, other, send_y, from_y, load_sem, down_load, down_send, down_recv, tok_send, tok_recv,
-           y_send, y_recv, part_send, part_recv, hid_send, hid_recv, sum_send, sum_recv, col_send, col_recv):
+           y_send, y_recv, part_send, part_recv, hid_send, hid_recv, sum_send, sum_recv, col_send, col_recv,
+           done, land, passed, out_send, out_recv, pass_send, pass_recv):
     row, col, core = lax.axis_index("row"), lax.axis_index("col"), lax.axis_index("depth")
     half = n // 2
     x, z = row % 2, row // 2
@@ -45,7 +46,16 @@
     barrier = pltpu.get_barrier_semaphore()
     for peer in ways + (beside, partner):
         pl.semaphore_signal(barrier, inc=1, device_id=peer, device_id_type=MESH)
-    pl.semaphore_wait(barrier, 4)
+    near = 1 - jnp.minimum((z // 2 - core) * (z // 2 - core) + (z % 2 - core) * (z % 2 - core), 1)
+    sinks = [{"row": 4 * core + m, "depth": z % 2} for m in range(4)]
+    feeds = [{"row": 4 * (m // 2) + 2 * core + m % 2, "depth": z // 2} for m in range(4)]
+    away = [(row - peer["row"]) * (row - peer["row"]) + (core - peer["depth"]) * (core - peer["depth"])
+            for peer in sinks + feeds]
+    for peer, far in zip(sinks + feeds, away):
+        @pl.when(far > 0)
+        def _(peer=peer):
+            pl.semaphore_signal(barrier, inc=1, device_id=peer, device_id_type=MESH)
+    pl.semaphore_wait(barrier, 12 - 2 * near)
     for copy in loads[:3]:
         copy.wait()
 
@@ -182,28 +192,63 @@
     for number in range(half, 2 * half + 1):
         wave(number)
 
-    few = n // 4
-
-    def sum_copy(side, k):
+    part_rows = block // 2
+
+    def rows_in(c):
+        return pl.ds(pl.multiple_of(c * part_rows, part_rows), part_rows)
+
+    def sum_copy(side, m):
         c = 1 - col if side == 0 else col
-        return remote(total.at[(c * 2 + 1 - core) * few + k], other.at[side, k],
-                      sum_send.at[side, k], sum_recv.at[side, k], partner)
-
-    def col_copy(k):
-        return remote(send_y.at[k], from_y.at[k], col_send.at[k], col_recv.at[k], beside)
+        return remote(total.at[4 * (1 - core) + m, rows_in(c)], other.at[side, m],
+                      sum_send.at[side, m], sum_recv.at[side, m], partner)
+
+    def col_copy(m):
+        return remote(send_y.at[m], from_y.at[m], col_send.at[m], col_recv.at[m], beside)
+
+    spot = z // 2 * 2 + x
+
+    def out_copy(m):
+        return remote(done.at[m], land.at[spot], out_send.at[m], out_recv.at[spot], sinks[m])
+
+    def landed(at):
+        remote(done.at[0], land.at[at], out_send.at[0], out_recv.at[at], beside).wait_recv()
+
+    def pass_copy(k):
+        return remote(land.at[(1 - col) * 2 + k], passed.at[k], pass_send.at[k], pass_recv.at[k], beside)
 
     for side in (0, 1):
-        for k in range(few):
-            go(sum_copy(side, k))
-    for k in range(few):
-        sum_copy(0, k).wait_recv()
-        send_y[k] = (total[((1 - col) * 2 + core) * few + k] + other[0, k]).astype(BF16)
-        go(col_copy(k))
-    for k in range(few):
-        sum_copy(1, k).wait_recv()
-        mine = total[(col * 2 + core) * few + k] + other[1, k]
-        col_copy(k).wait_recv()
-        out_ref[k * block:(k + 1) * block] = (mine + from_y[k].astype(F32)).astype(BF16)
+        for m in range(4):
+            go(sum_copy(side, m))
+    for m in range(4):
+        sum_copy(0, m).wait_recv()
+        send_y[m] = (total[4 * core + m, rows_in(1 - col)] + other[0, m]).astype(BF16)
+        go(col_copy(m))
+    for m in range(4):
+        sum_copy(1, m).wait_recv()
+        mine = total[4 * core + m, rows_in(col)] + other[1, m]
+        col_copy(m).wait_recv()
+        done[m] = (mine + from_y[m].astype(F32)).astype(BF16)
+
+        @pl.when(away[m] > 0)
+        def _():
+            out_copy(m).start()
+
+        @pl.when(away[m] == 0)
+        def _():
+            pltpu.make_async_copy(done.at[m], land.at[spot], out_recv.at[spot]).start()
+    for k in (0, 1):
+        landed((1 - col) * 2 + k)
+        go(pass_copy(k))
+    for k in (0, 1):
+        landed(col * 2 + k)
+        out_ref[k, rows_in(col)] = land[col * 2 + k]
+    for k in (0, 1):
+        pass_copy(k).wait_recv()
+        out_ref[k, rows_in(1 - col)] = passed[k]
+    for m in range(4):
+        @pl.when(away[m] > 0)
+        def _():
+            out_copy(m).wait_send()
     for copy in started:
         copy.wait_send()
 
@@ -212,13 +257,13 @@
     block, width = tokens.shape
     units = gate_weight.shape[0]
     features = down_weight.shape[1]
-    few = n // 4
+    piece = block // 2
     half, share = n // 2, units // 2
     every = n * block
     dma = pltpu.SemaphoreType.DMA
     return pl.pallas_call(
         functools.partial(kernel, n),
-        out_shape=jax.ShapeDtypeStruct((every // 4, features), BF16),
+        out_shape=jax.ShapeDtypeStruct((2, block, features), BF16),
         in_specs=[pl.BlockSpec(memory_space=pl.ANY)] * 4,
         out_specs=pl.BlockSpec(memory_space=pltpu.VMEM),
         scratch_shapes=[
@@ -231,17 +276,21 @@
             pltpu.VMEM((half + 1, 2, share, 2 * block), F32),
             pltpu.VMEM((n, share, every), BF16),
             pltpu.VMEM((n, block, features), F32),
-            pltpu.VMEM((2, few, block, features), F32),
-            pltpu.VMEM((few, block, features), BF16),
-            pltpu.VMEM((few, block, features), BF16),
+            pltpu.VMEM((2, 4, piece, features), F32),
+            pltpu.VMEM((4, piece, features), BF16),
+            pltpu.VMEM((4, piece, features), BF16),
             dma((6,)),
             dma((half,)), dma((half,)), dma((half,)),
             dma((2, half, 2)), dma((2, half, 2)),
             dma((n,)), dma((n,)),
             dma((half + 1,)), dma((half + 1,)),
             dma((2, half, half)), dma((2, half, half)),
-            dma((2, few)), dma((2, few)),
-            dma((few,)), dma((few,)),
+            dma((2, 4)), dma((2, 4)),
+            dma((4,)), dma((4,)),
+            pltpu.VMEM((4, piece, features), BF16),
+            pltpu.VMEM((4, piece, features), BF16),
+            pltpu.VMEM((2, piece, features), BF16),
+            dma((4,)), dma((4,)), dma((2,)), dma((2,)),
         ],
         compiler_params=pltpu.CompilerParams(
             collective_id=0, has_side_effects=True, vmem_limit_bytes=60 * 1024 * 1024
@@ -289,7 +338,7 @@
         return send_out(mine.astype(BF16), rows, cols, depths)
 
     def fused(*args):
-        return send_out(partial_sums(rows, *args), rows, cols, depths)
+        return jnp.concatenate(list(partial_sums(rows, *args)), axis=1)
 
     in_specs = (
         P("row", "depth"),
@@ -298,5 +347,5 @@
         P(("col", "depth"), "row"),
     )
     out_specs = P("row", ("col", "depth"))
-    small = cols == 2 and depths == 2 and rows % 4 == 0
+    small = cols == 2 and depths == 2 and rows == 8
     return jax.shard_map(fused if small else local, mesh=mesh, in_specs=in_specs, out_specs=out_specs, check_vma=False)

time: 125 us -> 113 us (0.904)
  the two profiles are of different devices: /device:TPU:6 before, /device:TPU:10 now
where the time goes in v4:
time: 113 us
  Pallas kernels  111 us (98%)
  local copies, waits for them, and re-layouts  1.96 us (2%)
    pallas_call x1, Pallas kernels, partial_sums(): pl.pallas_call(functools.partial(kernel, n), out_shape=jax.ShapeDtypeStru...  111 us

profile of v4, /device:TPU:10, one launch (start us, length us, event | category | flops | bytes accessed | tf_op | source)
XLA Modules:
  0.0 112.8 jit_solution(17394847550342655836)
XLA Ops:
  0.0 110.7 %shard_map.46 = bf16[2,128,672]{2,1,0:T(8,128)(2,1)} custom-call(bf16[128,2688]{1,0:T(8,128)(2,1)} %tok_hbm.1, bf16[576,2688]{1,0:T(8,128)(2,1)} %gate_hbm.1, bf16[576,2688]{1,0:T(8,128)(2,1)} %up_hbm.1, bf16[672,2304]{1,0:T(8,128)(2,1)} %bitcast.5), custom_call_target="tpu_custom_call" | custom-call | tf_op jit(solution)/shard_map/pallas_call | solution.py:264
  110.7 1.0 slice_bitcast_fusion.1
  111.7 0.1 pad_maximum_fusion
  111.9 0.9 copy.5
